TPU v7x, 512 devices: a whole 4x4x16 slice. The times are simulated.
512 devices in a mesh: row: 16 (over y_hi, x, core), col: 32 (over z, y_lo).
Axes of the slice: x: 4, y: 4 (y_hi: 2, y_lo: 2; y = y_hi * 2 + y_lo), z: 16, core: 2. Of those that a mesh axis runs over, the one named last changes fastest.
Arguments:
- specimen: float32 [2, 2048, 8192], P(None, 'row', 'col'), may hold values from -6 to 6
- probe_field: float32 [2, 256, 256], replicated, may hold values from -6 to 6
- scan_offsets: int32 [16, 32, 2, 2], replicated, may hold values from -128 to 128, as said below
- live_counts: int32 [16, 32], replicated, may hold values from 1 to 2, as said below
- magnitudes: float32 [16, 32, 2, 256, 256], P('row', 'col'), may hold values from 0 to 2
Outputs:
- specimen_next: float32 [2, 2048, 8192], P(None, 'row', 'col')
- probe_next: float32 [2, 256, 256], replicated
Inputs may be any that keep to these rules, and one draw needn't show every extreme that they name: `scan_offsets`: rows of a patch start within -128 to 0 of the tile's first row, columns within -128 to 128 of its first column. Tile (a, b) owns the positions in its first live_counts[a, b] slots.
All inputs are finite; a program needn't handle non-finite values.
Results may differ from a plain program's by a relative error of at most 0.0003.
Values sent between devices are 32-bit elements; how exact they have to be, the bound alone decides.
A program may use at most 64 MiB of HBM per device.

v0:
```python
import math
import jax
import jax.numpy as jnp
from jax import lax
from jax.sharding import PartitionSpec as P

modulus_floor = 0.25
object_damping = 0.1
probe_damping = 0.1


def extended_2(block, sides, width):
    for axis, dim in sides:
        count = lax.axis_size(axis)
        forward = [(i, i + 1) for i in range(count - 1)]
        backward = [(target, source) for source, target in forward]
        low = lax.ppermute(
            lax.slice_in_dim(block, block.shape[dim] - width, None, axis=dim), axis, forward
        )
        high = lax.ppermute(lax.slice_in_dim(block, 0, width, axis=dim), axis, backward)
        block = jnp.concatenate([low, block, high], axis=dim)
    return block


def dft_tables(width):
    counter = jnp.arange(width, dtype=jnp.int32)
    phase = counter[:, None] * counter[None, :] % width
    angle = phase.astype(jnp.float32) * (2.0 * math.pi / width)
    factor = 1.0 / math.sqrt(width)
    return (jnp.cos(angle) * factor, jnp.sin(angle) * factor)


def matmul_right(left, table):
    return jnp.einsum("sjm,ml->sjl", left, table, precision=lax.Precision.HIGHEST)


def matmul_left(table, right):
    return jnp.einsum("kj,sjl->skl", table, right, precision=lax.Precision.HIGHEST)


def transform(wave_real, wave_imag, cosine, sine, direction):
    inner_real = matmul_right(wave_real, cosine) + direction * matmul_right(wave_imag, sine)
    inner_imag = matmul_right(wave_imag, cosine) - direction * matmul_right(wave_real, sine)
    outer_real = matmul_left(cosine, inner_real) + direction * matmul_left(sine, inner_imag)
    outer_imag = matmul_left(cosine, inner_imag) - direction * matmul_left(sine, inner_real)
    return (outer_real, outer_imag)


def fold_rims(wide, tile_r, tile_c, half):
    center = wide[:, 2 * half : 2 * half + tile_r, :]
    center = center.at[:, :half, :].add(wide[:, :half, :])
    center = center.at[:, tile_r - half :, :].add(wide[:, tile_r + 3 * half :, :])
    result = center[:, :, 2 * half : 2 * half + tile_c]
    result = result.at[:, :, :half].add(center[:, :, :half])
    result = result.at[:, :, tile_c - half :].add(center[:, :, tile_c + 3 * half :])
    return result


def shards(specimen, probe_field, scan_offsets, live_counts, magnitudes):
    width = probe_field.shape[1]
    half = width // 2
    tile_r = specimen.shape[1]
    tile_c = specimen.shape[2]
    slots = magnitudes.shape[2]
    row_place = lax.axis_index("row")
    col_place = lax.axis_index("col")
    zero_index = jnp.zeros((), jnp.int32)
    extended = extended_2(specimen, (("row", 1), ("col", 2)), half)
    offsets_here = scan_offsets[row_place, col_place]
    live = (jnp.arange(slots, dtype=jnp.int32) < live_counts[row_place, col_place]).astype(
        jnp.float32
    )[:, None, None]
    row_starts = offsets_here[:, 0] + half
    col_starts = offsets_here[:, 1] + half

    def extract(row_start, col_start):
        return lax.dynamic_slice(extended, (zero_index, row_start, col_start), (2, width, width))

    patches = jax.vmap(extract)(row_starts, col_starts)
    patch_real = patches[:, 0]
    patch_imag = patches[:, 1]
    probe_real = probe_field[0]
    probe_imag = probe_field[1]
    power = probe_real * probe_real + probe_imag * probe_imag
    cosine, sine = dft_tables(width)
    wave_real = probe_real * patch_real - probe_imag * patch_imag
    wave_imag = probe_real * patch_imag + probe_imag * patch_real
    far_real, far_imag = transform(wave_real, wave_imag, cosine, sine, 1.0)
    modulus = jnp.sqrt(far_real * far_real + far_imag * far_imag)
    factor = magnitudes[0, 0] / jnp.maximum(modulus, modulus_floor) - 1.0
    diff_real, diff_imag = transform(far_real * factor, far_imag * factor, cosine, sine, -1.0)
    diff_real = diff_real * live
    diff_imag = diff_imag * live
    grad_real = probe_real * diff_real + probe_imag * diff_imag
    grad_imag = probe_real * diff_imag - probe_imag * diff_real
    pieces = jnp.stack([grad_real, grad_imag, live * power], axis=1)
    layers = pieces.shape[1]

    def place(slot, total):
        start = (zero_index, row_starts[slot], col_starts[slot])
        current = lax.dynamic_slice(total, start, (layers, width, width))
        return lax.dynamic_update_slice(total, current + pieces[slot], start)

    start_total = jnp.zeros((layers, tile_r + 2 * half, tile_c + 2 * half), jnp.float32)
    buffer = lax.fori_loop(0, slots, place, start_total)
    wide = extended_2(buffer, (("row", 1), ("col", 2)), half)
    folded = fold_rims(wide, tile_r, tile_c, half)
    update = folded[:2]
    lighting = folded[2]
    damping = object_damping * jnp.max(power)
    specimen_next = specimen + update / (lighting + damping)
    local_terms = (
        jnp.sum(patch_real * diff_real + patch_imag * diff_imag, 0),
        jnp.sum(patch_real * diff_imag - patch_imag * diff_real, 0),
        jnp.sum(live * (patch_real * patch_real + patch_imag * patch_imag), 0),
    )
    sum_real, sum_imag, weight = lax.psum(
        (local_terms[0], local_terms[1], local_terms[2]), ("row", "col")
    )
    denominator = weight + probe_damping * jnp.mean(weight)
    probe_next = probe_field + jnp.stack([sum_real, sum_imag]) / denominator
    return (specimen_next, probe_next)


def solution(mesh):
    return jax.shard_map(
        shards,
        mesh=mesh,
        in_specs=(P(None, "row", "col"), P(), P(), P(), P("row", "col", None, None, None)),
        out_specs=(P(None, "row", "col"), P()),
        check_vma=False,
    )
```

profile of v0, /device:TPU:8, one launch (start us, length us, event | category | flops | bytes accessed | tf_op | source)
XLA Modules:
  0.0 654.2 jit_solution(3833202811847272772)
XLA Ops:
  7.2 1.9 collective-permute-start
  9.1 1.3 collective-permute-start.1
  10.4 1.1 slice_bitcast_fusion.1
  11.5 0.2 dynamic-slice_reduce_fusion
  11.9 1.3 dynamic_slice.35
  13.3 0.7 collective-permute-done.1
  14.1 1.0 fusion.148
  15.0 3.7 collective-permute-start.2
  18.7 4.1 collective-permute-start.3
  22.9 0.7 compare_convert_fusion
  23.6 1.0 copy.32
  24.7 13.0 %collective-permute-done.2 = f32[2,384,128]{2,1,0:T(8,128)S(1)} collective-permute-done((f32[2,384,128]{2,1,0:T(8,128)}, f32[2,384,128]{2,1,0:T(8,128)S(1)}, u32[]{:S(2)}, u32[]{:S(2)}) %collective-permute-start.2) | collective-permute-done | bytes 393248 | tf_op jit(solution)/shard_map/ppermute | solution.py:17
  37.7 0.8 copy-done.9
  38.5 1.3 pad_maximum_fusion
  39.7 5.8 while.21
  39.8 0.6 fusion.164
  40.4 2.3 bitcast_dynamic-update-slice_fusion.2
  42.7 0.6 fusion.164
  43.3 2.2 bitcast_dynamic-update-slice_fusion.2
  45.6 2.9 fusion.49
  48.5 1.6 fusion.53
  50.0 1.6 convolution_subtract_fusion.1
  51.6 1.8 fusion.47
  53.5 1.6 convolution_add_fusion.1
  55.1 1.8 fusion.51
  56.9 2.0 fusion.8
  58.9 2.0 fusion.25
  60.9 1.6 fusion.41
  62.5 1.6 fusion.45
  64.2 1.7 fusion.5
  65.8 1.7 fusion.6
  67.5 1.6 fusion.43
  69.1 2.6 fusion.39
  71.7 2.4 fusion.4
  74.1 1.2 copy.44
  75.3 4.0 fusion.16
  79.3 1.3 pad_maximum_fusion.1
  80.6 0.3 broadcast_in_dim.2
  80.8 34.3 %while.20 = (s32[]{:T(128)}, f32[3,384,512]{2,1,0:T(8,128)S(1)}, s32[2]{0:T(128)S(1)}, s32[2]{0:T(128)S(1)}, f32[2,3,256,256]{3,2,0,1:T(8,128)}, /*index=5*/s32[]{:T(128)}, s32[]{:T(128)}, s32[]{:T(128)}, s32[]{:T(128)}) while((s32[]{:T(128)}, f32[3,384,512]{2,1,0:T(8,128)S(1)}, s32[2]{0:T(128)S(1)}, s32[2]{0:T(128)S(1)}, ...), condition=%wide.region_1.2_spmd, body=%wide.region_0.1_spmd.sunk | while | flops 196616 | bytes 3932361 | solution.py:105
  80.9 0.7 dynamic_slice.46
  83.4 0.7 dynamic_slice.45
  86.0 1.4 bitcast_add_fusion.2
  87.4 10.8 %dynamic_update_slice.8 = f32[3,384,512]{2,1,0:T(8,128)S(1)} dynamic-update-slice(f32[3,384,512]{2,1,0:T(8,128)S(1)} %get-tuple-element.311, f32[3,256,256]{2,1,0:T(8,128)S(1)} %bitcast_add_fusion.2, s32[]{:T(128)} %constant.194.clone.1..sunk, s32[]{:T(128)S(6)} %select_n.146, s32[]{:T(128)S(6)} %select_n.147) | dynamic-update-slice | bytes 1572868 | tf_op jit(solution)/shard_map/while/body/eval_jaxpr/dynamic_update_slice | solution.py:102
  98.3 0.7 dynamic_slice.46
  100.8 0.7 dynamic_slice.45
  103.4 1.4 bitcast_add_fusion.2
  104.8 10.4 %dynamic_update_slice.8 = f32[3,384,512]{2,1,0:T(8,128)S(1)} dynamic-update-slice(f32[3,384,512]{2,1,0:T(8,128)S(1)} %get-tuple-element.311, f32[3,256,256]{2,1,0:T(8,128)S(1)} %bitcast_add_fusion.2, s32[]{:T(128)} %constant.194.clone.1..sunk, s32[]{:T(128)S(6)} %select_n.146, s32[]{:T(128)S(6)} %select_n.147) | dynamic-update-slice | bytes 1572868 | tf_op jit(solution)/shard_map/while/body/eval_jaxpr/dynamic_update_slice | solution.py:102
  115.3 8.6 %collective-permute-start.4 = (f32[3,128,512]{2,1,0:T(8,128)S(1)}, f32[3,128,512]{2,1,0:T(8,128)S(1)}, u32[]{:S(2)}, u32[]{:S(2)}) collective-permute-start(f32[3,128,512]{2,1,0:T(8,128)S(1)} %get-tuple-element.210), channel_id=1, source_target_pairs={{0,32},{32,64},{64,96},{96,128},{128,160},{160,192},{192,224},{224... | collective-permute-start | bytes 2359304 | tf_op jit(solution)/shard_map/ppermute | solution.py:17
  124.0 1.3 collective-permute-start.5
  125.3 0.5 collective-permute-done.4
  126.1 3.6 collective-permute-done.5
  129.7 1.1 fusion.146
  130.8 1.1 copy-done.1
  131.9 2.4 collective-permute-start.6
  134.3 3.5 collective-permute-start.7
  137.8 0.7 add_reduce_fusion
  139.3 498.2 %all-reduce.3.cloned.1.call-done = (f32[1,256,256]{2,1,0:T(8,128)}, f32[1,256,256]{2,1,0:T(8,128)}, f32[256,256]{1,0:T(8,128)}) async-done(((f32[1,256,256]{2,1,0:T(8,128)}, f32[1,256,256]{2,1,0:T(8,128)}, f32[256,256]{1,0:T(8,128)}), (f32[1,256,256]{2,1,0:T(8,128)}, f32[1,256,256]{2,1,0:T(8,128)}, f32[256,256]{1,0:T(8,128)})) %all-reduce.3.cloned.1.call-update) | async-done | bytes 786448 | tf_op jit(solution)/shard_map/psum | solution.py:117
  637.5 1.6 reduce_sum.39
  639.8 1.0 broadcast_add_fusion
  640.8 1.9 fusion.10
  642.7 1.9 fusion.9
  644.7 0.8 copy-done.2
  645.7 0.8 copy-done.6
  646.6 0.7 fusion.30
  (40 shorter events, 1.2 us)
Async XLA Ops:
  7.2 4.4 copy-start
  7.2 6.1 copy-start.5
  7.2 630.3 %all-reduce.3.cloned.1.call-start = ((), (), s32[]{:S(2)}) async-start(), calls=%async_computation | async-start | bytes 1572864 | tf_op jit(solution)/shard_map/psum | solution.py:117
  7.2 6.0 collective-permute-start
  9.1 4.9 collective-permute-start.1
  13.2 10.3 %copy-start.7 = (f32[1,1,2,256,256]{4,3,2,1,0:T(8,128)S(1)}, f32[1,1,2,256,256]{4,3,2,1,0:T(8,128)}, u32[]{:S(2)}) copy-start(f32[1,1,2,256,256]{4,3,2,1,0:T(8,128)} %param.23) | copy-start | bytes 1572868
  15.0 22.7 %collective-permute-start.2 = (f32[2,384,128]{2,1,0:T(8,128)}, f32[2,384,128]{2,1,0:T(8,128)S(1)}, u32[]{:S(2)}, u32[]{:S(2)}) collective-permute-start(f32[2,384,128]{2,1,0:T(8,128)} %get-tuple-element.217), channel_id=1, source_target_pairs={{0,1},{1,2},{2,3},{3,4},{4,5},{5,6},{6,7},{7,8},{8,9},{9,10},{10,1... | collective-permute-start | bytes 1179656 | tf_op jit(solution)/shard_map/ppermute | solution.py:17
  18.7 19.7 %collective-permute-start.3 = (f32[2,384,128]{2,1,0:T(8,128)}, f32[2,384,128]{2,1,0:T(8,128)}, u32[]{:S(2)}, u32[]{:S(2)}) collective-permute-start(f32[2,384,128]{2,1,0:T(8,128)} %get-tuple-element.218), channel_id=1, source_target_pairs={{1,0},{2,1},{3,2},{4,3},{5,4},{6,5},{7,6},{8,7},{9,8},{10,9},{11,1... | collective-permute-start | bytes 1179656 | tf_op jit(solution)/shard_map/ppermute | solution.py:20
  37.7 0.8 copy-start.9
  45.6 2.9 copy-start.4
  55.1 3.8 copy-start.8
  115.3 10.5 %collective-permute-start.4 = (f32[3,128,512]{2,1,0:T(8,128)S(1)}, f32[3,128,512]{2,1,0:T(8,128)S(1)}, u32[]{:S(2)}, u32[]{:S(2)}) collective-permute-start(f32[3,128,512]{2,1,0:T(8,128)S(1)} %get-tuple-element.210), channel_id=1, source_target_pairs={{0,32},{32,64},{64,96},{96,128},{128,160},{160,192},{192,224},{224... | collective-permute-start | bytes 2359304 | tf_op jit(solution)/shard_map/ppermute | solution.py:17
  124.0 5.7 collective-permute-start.5
  129.7 2.2 copy-start.1
  129.7 8.1 %copy-start.3 = (f32[2,256,256]{2,1,0:T(8,128)S(1)}, f32[2,256,256]{2,1,0:T(8,128)}, u32[]{:S(2)}) copy-start(f32[2,256,256]{2,1,0:T(8,128)} %param.20) | copy-start | bytes 1572868
  131.9 510.8 %collective-permute-start.6 = (f32[3,640,128]{2,1,0:T(8,128)}, f32[3,640,128]{2,1,0:T(8,128)S(1)}, u32[]{:S(2)}, u32[]{:S(2)}) collective-permute-start(f32[3,640,128]{2,1,0:T(8,128)} %get-tuple-element.207), channel_id=1, source_target_pairs={{0,1},{1,2},{2,3},{3,4},{4,5},{5,6},{6,7},{7,8},{8,9},{9,10},{10,1... | collective-permute-start | bytes 2949128 | tf_op jit(solution)/shard_map/ppermute | solution.py:17
  134.3 508.4 %collective-permute-start.7 = (f32[3,640,128]{2,1,0:T(8,128)S(1)}, f32[3,640,128]{2,1,0:T(8,128)S(1)}, u32[]{:S(2)}, u32[]{:S(2)}) collective-permute-start(f32[3,640,128]{2,1,0:T(8,128)S(1)} %get-tuple-element.208), channel_id=1, source_target_pairs={{1,0},{2,1},{3,2},{4,3},{5,4},{6,5},{7,6},{8,7},{9,8},{10,9},{11,1... | collective-permute-start | bytes 2949128 | tf_op jit(solution)/shard_map/ppermute | solution.py:20
  642.7 2.8 copy-start.2
  645.6 1.0 copy-start.6
Sparse Core Ops, SparseCore 0:
  138.0 499.5 all-reduce.2
where the time goes:
time: 655 us; the launch traced here: 654 us
  waiting for transfers between devices  516 us (79%)
  local copies, waits for them, and re-layouts  39.8 us (6%)
  matrix products  32.3 us (5%)
  starting transfers between devices  26.8 us (4%)
  between operations  15.8 us (2%)
  other arithmetic  15.6 us (2%)
  loops' own time  7.67 us (1%)
    psum x1, waiting for transfers between devices, shards(): lax.psum((local_terms[0], local_terms[1], local_terms[2]), ('row', 'col'))  498 us
    dynamic_update_slice x2, local copies, waits for them, and re-layouts, place(): return lax.dynamic_update_slice(total, current + pieces[slot], start)  21.2 us
    dot_general x8, matrix products, matmul_left(): jnp.einsum('kj,sjl->skl', table, right, precision=lax.Precision.HIGHEST)  18.1 us
    ppermute x4, starting transfers between devices, extended_2(): lax.ppermute(lax.slice_in_dim(block, block.shape[dim] - width, None, axis...  16.6 us
    dot_general x8, matrix products, matmul_right(): jnp.einsum('sjm,ml->sjl', left, table, precision=lax.Precision.HIGHEST)  14.2 us
    ppermute x4, waiting for transfers between devices, extended_2(): lax.ppermute(lax.slice_in_dim(block, block.shape[dim] - width, None, axis...  13.5 us
  transfers between devices with their start and end apart: 9, of which 5 were waited for; matrix products, arithmetic and copies ran while one was open for 2% of the time, Pallas kernels for 0%

commit v1 on v0

--- a/solution.py
+++ b/solution.py
@@ -57,6 +57,10 @@
 
 
 def shards(specimen, probe_field, scan_offsets, live_counts, magnitudes):
+
+    def build_the_sample(mesh_ax, along_axis, own_rows):
+        return jax.lax.psum(jax.lax.psum(own_rows, axis_name=mesh_ax), axis_name=along_axis)
+
     width = probe_field.shape[1]
     half = width // 2
     tile_r = specimen.shape[1]
@@ -114,8 +118,8 @@
         jnp.sum(patch_real * diff_imag - patch_imag * diff_real, 0),
         jnp.sum(live * (patch_real * patch_real + patch_imag * patch_imag), 0),
     )
-    sum_real, sum_imag, weight = lax.psum(
-        (local_terms[0], local_terms[1], local_terms[2]), ("row", "col")
+    sum_real, sum_imag, weight = build_the_sample(
+        "col", "row", (local_terms[0], local_terms[1], local_terms[2])
     )
     denominator = weight + probe_damping * jnp.mean(weight)
     probe_next = probe_field + jnp.stack([sum_real, sum_imag]) / denominator

time: 655 us -> 580 us (0.89)
  the two profiles are of different devices: /device:TPU:8 before, /device:TPU:1 now
where the time goes in v1:
time: 580 us; the launch traced here: 579 us
  waiting for transfers between devices  439 us (76%)
  local copies, waits for them, and re-layouts  46.1 us (8%)
  matrix products  32.4 us (6%)
  starting transfers between devices  22.1 us (4%)
  between operations  15.8 us (3%)
  other arithmetic  15.5 us (3%)
  loops' own time  8.34 us (1%)
    psum x1, waiting for transfers between devices, build_the_sample(): jax.lax.psum(own_rows, axis_name=mesh_ax)  246 us
    psum x1, waiting for transfers between devices, build_the_sample(): jax.lax.psum(jax.lax.psum(own_rows, axis_name=mesh_ax), axis_name=along_a...  181 us
    dynamic_update_slice x2, local copies, waits for them, and re-layouts, place(): return lax.dynamic_update_slice(total, current + pieces[slot], start)  25.3 us
    dot_general x8, matrix products, matmul_left(): jnp.einsum('kj,sjl->skl', table, right, precision=lax.Precision.HIGHEST)  18.1 us
    dot_general x8, matrix products, matmul_right(): jnp.einsum('sjm,ml->sjl', left, table, precision=lax.Precision.HIGHEST)  14.3 us
    ppermute x4, waiting for transfers between devices, extended_2(): lax.ppermute(lax.slice_in_dim(block, block.shape[dim] - width, None, axis...  12.7 us
  transfers between devices with their start and end apart: 10, of which 3 were waited for; matrix products, arithmetic and copies ran while one was open for 2% of the time, Pallas kernels for 0%

profile of v1, /device:TPU:1, one launch (start us, length us, event | category | flops | bytes accessed | tf_op | source)
XLA Modules:
  0.0 579.4 jit_solution(15719513567809880462)
XLA Ops:
  7.2 4.6 collective-permute-start
  11.9 5.6 collective-permute-start.1
  17.4 1.1 slice_bitcast_fusion.1
  18.6 0.2 dynamic-slice_reduce_fusion
  19.0 1.3 dynamic_slice.35
  20.3 1.0 fusion.148
  21.3 2.7 collective-permute-start.2
  24.0 1.3 collective-permute-start.3
  25.3 0.7 compare_convert_fusion
  26.0 1.0 copy.32
  27.2 12.7 %collective-permute-done.2 = f32[2,384,128]{2,1,0:T(8,128)S(1)} collective-permute-done((f32[2,384,128]{2,1,0:T(8,128)}, f32[2,384,128]{2,1,0:T(8,128)S(1)}, u32[]{:S(2)}, u32[]{:S(2)}) %collective-permute-start.2) | collective-permute-done | bytes 393248 | tf_op jit(solution)/shard_map/ppermute | solution.py:17
  39.8 0.8 copy-done.9
  40.6 1.3 pad_maximum_fusion
  41.9 5.7 while.21
  41.9 0.6 fusion.164
  42.5 2.2 bitcast_dynamic-update-slice_fusion.2
  44.8 0.6 fusion.164
  45.4 2.2 bitcast_dynamic-update-slice_fusion.2
  47.6 2.9 fusion.49
  50.5 1.6 fusion.53
  52.1 1.6 convolution_subtract_fusion.1
  53.7 1.6 convolution_add_fusion.1
  55.3 1.8 fusion.51
  57.1 1.8 fusion.47
  58.9 2.0 fusion.8
  60.9 2.0 fusion.25
  62.9 1.7 fusion.41
  64.6 1.7 fusion.45
  66.2 1.7 fusion.5
  67.9 1.7 fusion.6
  69.6 1.6 fusion.43
  71.1 2.6 fusion.39
  73.8 2.4 fusion.4
  76.1 1.2 copy.44
  77.4 4.0 fusion.16
  81.4 1.3 pad_maximum_fusion.1
  82.6 0.3 broadcast_in_dim.2
  82.9 39.1 %while.20 = (s32[]{:T(128)}, f32[3,384,512]{2,1,0:T(8,128)S(1)}, s32[2]{0:T(128)S(1)}, s32[2]{0:T(128)S(1)}, f32[2,3,256,256]{3,2,0,1:T(8,128)}, /*index=5*/s32[]{:T(128)}, s32[]{:T(128)}, s32[]{:T(128)}, s32[]{:T(128)}) while((s32[]{:T(128)}, f32[3,384,512]{2,1,0:T(8,128)S(1)}, s32[2]{0:T(128)S(1)}, s32[2]{0:T(128)S(1)}, ...), condition=%wide.region_1.2_spmd, body=%wide.region_0.1_spmd.sunk | while | flops 196616 | bytes 3932361 | solution.py:109
  82.9 0.7 dynamic_slice.46
  85.6 0.7 dynamic_slice.45
  88.4 1.4 bitcast_add_fusion.2
  89.8 11.6 %dynamic_update_slice.8 = f32[3,384,512]{2,1,0:T(8,128)S(1)} dynamic-update-slice(f32[3,384,512]{2,1,0:T(8,128)S(1)} %get-tuple-element.314, f32[3,256,256]{2,1,0:T(8,128)S(1)} %bitcast_add_fusion.2, s32[]{:T(128)} %constant.194.clone.1..sunk, s32[]{:T(128)S(6)} %select_n.146, s32[]{:T(128)S(6)} %select_n.147) | dynamic-update-slice | bytes 1572868 | tf_op jit(solution)/shard_map/while/body/eval_jaxpr/dynamic_update_slice | solution.py:106
  101.5 0.7 dynamic_slice.46
  104.2 0.7 dynamic_slice.45
  106.9 1.4 bitcast_add_fusion.2
  108.4 13.6 %dynamic_update_slice.8 = f32[3,384,512]{2,1,0:T(8,128)S(1)} dynamic-update-slice(f32[3,384,512]{2,1,0:T(8,128)S(1)} %get-tuple-element.314, f32[3,256,256]{2,1,0:T(8,128)S(1)} %bitcast_add_fusion.2, s32[]{:T(128)} %constant.194.clone.1..sunk, s32[]{:T(128)S(6)} %select_n.146, s32[]{:T(128)S(6)} %select_n.147) | dynamic-update-slice | bytes 1572868 | tf_op jit(solution)/shard_map/while/body/eval_jaxpr/dynamic_update_slice | solution.py:106
  122.1 1.3 fusion.147
  123.3 1.9 collective-permute-start.4
  125.3 3.3 collective-permute-start.5
  128.5 246.0 %all-reduce.5.cloned.1.call-done = (f32[256,256]{1,0:T(8,128)}, f32[256,256]{1,0:T(8,128)}, f32[256,256]{1,0:T(8,128)}) async-done(((f32[256,256]{1,0:T(8,128)}, f32[256,256]{1,0:T(8,128)}, f32[256,256]{1,0:T(8,128)}), (f32[256,256]{1,0:T(8,128)}, f32[256,256]{1,0:T(8,128)}, f32[256,256]{1,0:T(8,128)})) %all-reduce.5.cloned.1.call-update) | async-done | bytes 786448 | tf_op jit(solution)/shard_map/psum | solution.py:62
  374.6 1.2 constant_dynamic-update-slice_fusion.5
  376.1 1.1 fusion.146
  377.2 1.1 copy-done.1
  378.3 1.4 collective-permute-start.6
  379.6 1.3 collective-permute-start.7
  381.0 0.7 add_reduce_fusion
  382.3 180.5 %all-reduce.7.cloned.1.call-done = (f32[1,256,256]{2,1,0:T(8,128)}, f32[1,256,256]{2,1,0:T(8,128)}, f32[256,256]{1,0:T(8,128)}) async-done(((f32[1,256,256]{2,1,0:T(8,128)}, f32[1,256,256]{2,1,0:T(8,128)}, f32[256,256]{1,0:T(8,128)}), (f32[1,256,256]{2,1,0:T(8,128)}, f32[1,256,256]{2,1,0:T(8,128)}, f32[256,256]{1,0:T(8,128)})) %all-reduce.7.cloned.1.call-update) | async-done | bytes 786448 | tf_op jit(solution)/shard_map/psum | solution.py:62
  562.8 1.6 reduce_sum.39
  565.1 1.0 broadcast_add_fusion
  566.1 1.9 fusion.10
  568.0 1.9 fusion.9
  569.9 0.8 copy-done.2
  571.0 0.8 copy-done.6
  571.9 0.7 fusion.30
  (43 shorter events, 1.1 us)
Async XLA Ops:
  7.2 11.4 %copy-start = (s32[16,32,2,2]{1,3,2,0:T(2,128)S(1)}, s32[16,32,2,2]{1,3,2,0:T(2,128)}, u32[]{:S(2)}) copy-start(s32[16,32,2,2]{1,3,2,0:T(2,128)} %param.21) | copy-start | bytes 24580
  7.2 13.1 %copy-start.5 = (f32[2,128,256]{2,1,0:T(8,128)S(1)}, f32[2,128,256]{2,1,0:T(8,128)}, u32[]{:S(2)}) copy-start(f32[2,128,256]{2,1,0:T(8,128)} %param.19) | copy-start | bytes 786436
  7.2 367.4 %all-reduce.5.cloned.1.call-start = ((), (), s32[]{:S(2)}) async-start(), calls=%async_computation | async-start | bytes 1572864 | tf_op jit(solution)/shard_map/psum | solution.py:62
  7.2 13.0 %collective-permute-start = (f32[2,128,256]{2,1,0:T(8,128)}, f32[2,128,256]{2,1,0:T(8,128)S(1)}, u32[]{:S(2)}, u32[]{:S(2)}) collective-permute-start(f32[2,128,256]{2,1,0:T(8,128)} %param.19), channel_id=1, source_target_pairs={{0,32},{32,64},{64,96},{96,128},{128,160},{160,192},{192,224},{224... | collective-permute-start | bytes 786440 | tf_op jit(solution)/shard_map/ppermute | solution.py:17
  11.9 8.4 %collective-permute-start.1 = (f32[2,128,256]{2,1,0:T(8,128)}, f32[2,128,256]{2,1,0:T(8,128)S(1)}, u32[]{:S(2)}, u32[]{:S(2)}) collective-permute-start(f32[2,128,256]{2,1,0:T(8,128)} %param.19), channel_id=1, source_target_pairs={{32,0},{64,32},{96,64},{128,96},{160,128},{192,160},{224,192},{256... | collective-permute-start | bytes 786440 | tf_op jit(solution)/shard_map/ppermute | solution.py:20
  20.2 5.7 copy-start.7
  21.3 18.5 %collective-permute-start.2 = (f32[2,384,128]{2,1,0:T(8,128)}, f32[2,384,128]{2,1,0:T(8,128)S(1)}, u32[]{:S(2)}, u32[]{:S(2)}) collective-permute-start(f32[2,384,128]{2,1,0:T(8,128)} %get-tuple-element.220), channel_id=1, source_target_pairs={{0,1},{1,2},{2,3},{3,4},{4,5},{5,6},{6,7},{7,8},{8,9},{9,10},{10,1... | collective-permute-start | bytes 1179656 | tf_op jit(solution)/shard_map/ppermute | solution.py:17
  24.0 16.6 %collective-permute-start.3 = (f32[2,384,128]{2,1,0:T(8,128)}, f32[2,384,128]{2,1,0:T(8,128)}, u32[]{:S(2)}, u32[]{:S(2)}) collective-permute-start(f32[2,384,128]{2,1,0:T(8,128)} %get-tuple-element.221), channel_id=1, source_target_pairs={{1,0},{2,1},{3,2},{4,3},{5,4},{6,5},{7,6},{8,7},{9,8},{10,9},{11,1... | collective-permute-start | bytes 1179656 | tf_op jit(solution)/shard_map/ppermute | solution.py:20
  39.8 0.8 copy-start.9
  47.6 2.9 copy-start.4
  57.1 3.8 copy-start.8
  122.0 440.8 %all-reduce.7.cloned.1.call-start = ((), (), s32[]{:S(2)}) async-start(), calls=%async_computation.1 | async-start | bytes 1572864 | tf_op jit(solution)/shard_map/psum | solution.py:62
  123.3 251.2 %collective-permute-start.4 = (f32[3,128,512]{2,1,0:T(8,128)}, f32[3,128,512]{2,1,0:T(8,128)}, u32[]{:S(2)}, u32[]{:S(2)}) collective-permute-start(f32[3,128,512]{2,1,0:T(8,128)} %get-tuple-element.213), channel_id=1, source_target_pairs={{0,32},{32,64},{64,96},{96,128},{128,160},{160,192},{192,224},{224... | collective-permute-start | bytes 2359304 | tf_op jit(solution)/shard_map/ppermute | solution.py:17
  125.3 250.7 %collective-permute-start.5 = (f32[3,128,512]{2,1,0:T(8,128)}, f32[3,128,512]{2,1,0:T(8,128)S(1)}, u32[]{:S(2)}, u32[]{:S(2)}) collective-permute-start(f32[3,128,512]{2,1,0:T(8,128)} %get-tuple-element.212), channel_id=1, source_target_pairs={{32,0},{64,32},{96,64},{128,96},{160,128},{192,160},{224,192},{256... | collective-permute-start | bytes 2359304 | tf_op jit(solution)/shard_map/ppermute | solution.py:20
  376.1 2.2 copy-start.1
  376.1 4.9 copy-start.3
  378.3 189.7 %collective-permute-start.6 = (f32[3,640,128]{2,1,0:T(8,128)}, f32[3,640,128]{2,1,0:T(8,128)S(1)}, u32[]{:S(2)}, u32[]{:S(2)}) collective-permute-start(f32[3,640,128]{2,1,0:T(8,128)} %get-tuple-element.210), channel_id=1, source_target_pairs={{0,1},{1,2},{2,3},{3,4},{4,5},{5,6},{6,7},{7,8},{8,9},{9,10},{10,1... | collective-permute-start | bytes 2949128 | tf_op jit(solution)/shard_map/ppermute | solution.py:17
  379.6 188.3 %collective-permute-start.7 = (f32[3,640,128]{2,1,0:T(8,128)S(1)}, f32[3,640,128]{2,1,0:T(8,128)S(1)}, u32[]{:S(2)}, u32[]{:S(2)}) collective-permute-start(f32[3,640,128]{2,1,0:T(8,128)S(1)} %get-tuple-element.211), channel_id=1, source_target_pairs={{1,0},{2,1},{3,2},{4,3},{5,4},{6,5},{7,6},{8,7},{9,8},{10,9},{11,1... | collective-permute-start | bytes 2949128 | tf_op jit(solution)/shard_map/ppermute | solution.py:20
  568.0 2.8 copy-start.2
  570.9 1.0 copy-start.6
Sparse Core Ops, SparseCore 0:
  122.1 252.3 all-reduce.4
  377.7 185.0 all-reduce.6
